TPU v7x, 128 devices: a whole 4x4x4 slice. The times are simulated.
128 devices in a mesh: dom: 32 (over z, y, core), col: 2 (over x_hi), batch: 2 (over x_lo).
Axes of the slice: x: 4 (x_hi: 2, x_lo: 2; x = x_hi * 2 + x_lo), y: 4, z: 4, core: 2. Of those that a mesh axis runs over, the one named last changes fastest.
Arguments:
- features: bfloat16 [65536, 128], P('dom', 'col'), may hold values from -6 to 6
- self_weight1: bfloat16 [128, 256], P('col', 'batch'), may hold values from -0.5 to 0.5
- neigh_weight1: bfloat16 [128, 256], P('col', 'batch'), may hold values from -2 to 2
- need_first: int32 [64, 64], P(('dom', 'batch')), may hold values from 0 to 511, as said below
- count_first: int32 [64], P(('dom', 'batch')), may hold values from 0 to 64
- adjacency_first: int32 [65536, 512], P(('dom', 'batch')), may hold values from 0 to 16384, as said below
- self_weight2: bfloat16 [256, 172], P('col', 'batch'), may hold values from -0.375 to 0.375
- neigh_weight2: bfloat16 [256, 172], P('col', 'batch'), may hold values from -0.375 to 0.375
- need_second: int32 [64, 64], P(('dom', 'batch')), may hold values from 0 to 511, as said below
- count_second: int32 [64], P(('dom', 'batch')), may hold values from 0 to 64
- adjacency_second: int32 [65536, 512], P(('dom', 'batch')), may hold values from 0 to 16384, as said below
- seed_rows: int32 [65536], P(('dom', 'batch')), may hold values from 0 to 2047
Outputs:
- logits: float32 [65536, 172], P(('dom', 'batch'))
Inputs may be any that keep to these rules, and one draw needn't show every extreme that they name: `need_first`: each row lists 64 different node blocks in increasing order; block g holds nodes 128 * g to 128 * g + 127 and lies in partition g // 16. At most 4 entries of one row lie in one partition, and exactly 4 lie in some partition in every row. `need_second`: each row lists 64 different frontier blocks in increasing order; block g holds frontier rows 128 * g to 128 * g + 127 and lies in partition g // 16. At most 4 entries of one row lie in one partition, and exactly 4 lie in some partition in every row. `adjacency_first`: bit i of word k of a row is the adjacency entry of column 16 k + i; at most one bit of a word is set, and bit 15 never. `adjacency_second`: bit i of word k of a row is the adjacency entry of column 16 k + i; at most one bit of a word is set, and bit 15 never.
All inputs are finite; a program needn't handle non-finite values.
Results may differ from a plain program's by a relative error of at most 0.0036.
Values may be sent and summed in bfloat16 or wider, within the bound.
A program may use at most 128 MiB of HBM per device.

v0:
```python
import math
import jax
import jax.numpy as jnp
from jax import lax
from jax.sharding import PartitionSpec as P

BLK = 128


def in_blocks(shard, dim, devices):
    shape = shard.shape
    blocks = shard.reshape(*shape[:dim], devices, shape[dim] // devices, *shape[dim + 1 :])
    return jnp.moveaxis(blocks, dim, 0)


def sent_and_summed(shard, axis, dim):
    devices = lax.axis_size(axis)
    blocks = lax.all_to_all(in_blocks(shard, dim, devices), axis, 0, 0, tiled=True)
    return jnp.sum(blocks, axis=0)


def from_everyone(shard, axis):
    copies = jnp.broadcast_to(shard, (lax.axis_size(axis), *shard.shape))
    return lax.all_to_all(copies, axis, split_axis=0, concat_axis=0, tiled=True)


def of_everyone(shard, axis):
    return from_everyone(shard, axis).sum(axis=0)


def unpack_rows(packed_rows, valid_cols):
    shifts = jnp.arange(16, dtype=jnp.int32)
    bit_table = jnp.right_shift(packed_rows[:, :, None], shifts[None, None, :]) & 1
    bit_table = bit_table.reshape(packed_rows.shape[0], packed_rows.shape[1] * 16)
    column = jnp.arange(bit_table.shape[1], dtype=jnp.int32)
    return jnp.where(column[None, :] < valid_cols, bit_table, 0)


def mean_rows(packed, valid_cols, needed):
    total_rows = packed.shape[0]
    row_block = math.gcd(total_rows, 256)
    grouped = packed.reshape(total_rows // row_block, row_block, packed.shape[1])

    def one_block(row_piece):
        dense_rows = unpack_rows(row_piece, valid_cols)
        degree = jnp.sum(dense_rows, axis=1).astype(jnp.float32)
        summed = jnp.dot(
            dense_rows.astype(jnp.bfloat16), needed, preferred_element_type=jnp.float32
        )
        return (summed / jnp.maximum(degree, 1.0)[:, None]).astype(jnp.bfloat16)

    return lax.map(one_block, grouped).reshape(total_rows, needed.shape[1])


def pick_blocks(holding, wanted, arriving):
    inside = (wanted >= 0) & (wanted < arriving.shape[0])
    taken_rows = jnp.take(arriving, jnp.clip(wanted, 0, arriving.shape[0] - 1), axis=0)
    return jnp.where(inside[:, None], taken_rows, holding)


def per_device(
    features,
    self_weight1,
    neigh_weight1,
    need_first,
    count_first,
    adjacency_first,
    self_weight2,
    neigh_weight2,
    need_second,
    count_second,
    adjacency_second,
    seed_rows,
):
    batch_at = lax.axis_index("batch")
    rows_first = adjacency_first.shape[0]
    node_blocks = features.reshape(features.shape[0] // BLK, BLK * features.shape[1])
    wanted_first = need_first[0]
    empty_first = jnp.zeros((wanted_first.shape[0], node_blocks.shape[1]), jnp.bfloat16)
    fetched_first = pick_blocks(
        empty_first, wanted_first, lax.all_gather(node_blocks, "dom", axis=0, tiled=True)
    )
    needed_first = fetched_first.reshape(-1, features.shape[1])
    near_first = mean_rows(adjacency_first, count_first[0] * BLK, needed_first)
    self_first = lax.dynamic_slice_in_dim(features, batch_at * rows_first, rows_first, 0)
    weight_self, weight_near = (
        lax.all_gather(self_weight1, "batch", axis=1, tiled=True),
        lax.all_gather(neigh_weight1, "batch", axis=1, tiled=True),
    )
    partial_first = jnp.dot(self_first, weight_self, preferred_element_type=jnp.float32) + jnp.dot(
        near_first, weight_near, preferred_element_type=jnp.float32
    )
    summed_first = sent_and_summed(partial_first, "col", 1)
    hidden_first = jnp.maximum(summed_first, 0.0).astype(jnp.bfloat16)
    frontier = lax.all_gather(hidden_first, "batch", axis=0, tiled=True)
    front_blocks = frontier.reshape(frontier.shape[0] // BLK, BLK * frontier.shape[1])
    wanted_second = need_second[0]
    empty_second = jnp.zeros((wanted_second.shape[0], front_blocks.shape[1]), jnp.bfloat16)
    fetched_second = pick_blocks(
        empty_second, wanted_second, lax.all_gather(front_blocks, "dom", axis=0, tiled=True)
    )
    needed_second = fetched_second.reshape(-1, frontier.shape[1])
    near_second = mean_rows(adjacency_second, count_second[0] * BLK, needed_second)
    own_second = jnp.take(frontier, seed_rows, axis=0)
    weight_own, weight_far = (
        lax.all_gather(self_weight2, "batch", axis=1, tiled=True),
        lax.all_gather(neigh_weight2, "batch", axis=1, tiled=True),
    )
    partial_second = jnp.dot(own_second, weight_own, preferred_element_type=jnp.float32) + jnp.dot(
        near_second, weight_far, preferred_element_type=jnp.float32
    )
    return of_everyone(partial_second, "col")


def solution(mesh):
    placed = (
        P("dom", "col"),
        P("col", "batch"),
        P("col", "batch"),
        P(("dom", "batch"), None),
        P(("dom", "batch")),
        P(("dom", "batch"), None),
        P("col", "batch"),
        P("col", "batch"),
        P(("dom", "batch"), None),
        P(("dom", "batch")),
        P(("dom", "batch"), None),
        P(("dom", "batch")),
    )
    return jax.shard_map(
        per_device, mesh=mesh, in_specs=placed, out_specs=P(("dom", "batch"), None), check_vma=False
    )
```

profile of v0, /device:TPU:0, one launch (start us, length us, event | category | flops | bytes accessed | tf_op | source)
XLA Modules:
  0.0 310.1 jit_solution(4355814135532355377)
XLA Ops:
  9.7 4.6 %all_gather.21 = bf16[64,256]{1,0:T(8,128)(2,1)S(1)} all-gather(bf16[64,128]{1,0:T(8,128)(2,1)} %param.17), channel_id=1, replica_groups=mesh['dom'=32,'col'=2,'batch'=2] {'batch'}, dimensions={1}, use_global_device_ids=true | all-gather | bytes 49152 | tf_op jit(solution)/shard_map/all_gather | solution.py:87
  14.3 4.6 %all_gather.23 = bf16[64,256]{1,0:T(8,128)(2,1)S(1)} all-gather(bf16[64,128]{1,0:T(8,128)(2,1)} %param.18), channel_id=1, replica_groups=mesh['dom'=32,'col'=2,'batch'=2] {'batch'}, dimensions={1}, use_global_device_ids=true | all-gather | bytes 49152 | tf_op jit(solution)/shard_map/all_gather | solution.py:88
  23.4 41.6 %all-gather.5.cloned.1.call-done = bf16[512,8192]{1,0:T(8,128)(2,1)} async-done(((bf16[16,8192]{1,0:T(8,128)(2,1)}), bf16[512,8192]{1,0:T(8,128)(2,1)}) %all-gather.5.cloned.1.call-update) | async-done | bytes 8388624 | tf_op jit(solution)/shard_map/all_gather | solution.py:81
  65.0 6.6 %gather_fusion = bf16[64,8192]{1,0:T(8,128)(2,1)S(1)} fusion(bf16[512,8192]{1,0:T(8,128)(2,1)} %all-gather.5.cloned.1.call-done, s32[1024]{0:T(1024)S(1)} %pad_clamp_fusion.1), kind=kCustom, calls=%fused_computation | custom fusion | bytes 2097408 | tf_op jit(solution)/shard_map/jit(_take)/gather | solution.py:57
  71.6 3.3 %gather.17 = bf16[8192,64]{1,0:T(8,128)(2,1)} reshape(bf16[64,8192]{1,0:T(8,128)(2,1)S(1)} %gather_fusion) | data formatting | bytes 2097152 | tf_op jit(solution)/shard_map/jit(_take)/gather | solution.py:57
  74.9 7.0 %select_select_fusion.1 = bf16[8192,64]{1,0:T(8,128)(2,1)S(1)} fusion(bf16[8192,64]{1,0:T(8,128)(2,1)} %gather.17, pred[8192]{0:T(1024)(128)(4,1)S(1)} %get-tuple-element.101, pred[8192]{0:T(1024)(128)(4,1)S(1)} %get-tuple-element.102), kind=kLoop, calls=%fused_computation.30 | loop fusion | flops 1048576 | bytes 2113536 | tf_op jit(solution)/shard_map/jit(_where)/select_n | solution.py:58
  81.9 36.0 %while.20 = (s32[]{:T(128)}, bf16[4,256,64]{1,2,0:T(8,128)(2,1)S(1)}, s32[]{:T(128)}, s32[4,256,512]{2,1,0:T(8,128)}, bf16[8192,64]{1,0:T(8,128)(2,1)S(1)}, /*index=5*/s32[]{:T(128)}) while((s32[]{:T(128)}, bf16[4,256,64]{1,2,0:T(8,128)(2,1)S(1)}, s32[]{:T(128)}, s32[4,256,512]{2,1,0:T(8,128)}, bf16[8192,64]{1,0:T(8,128)(2,1)S(1)}, ...), condition=%wide.region_2.3_spmd, body=%wide.region_0.2_spmd.sunk | while | flops 285278464 | bytes 13832277 | solution.py:52
  83.4 2.8 fusion.43
  86.2 3.6 %select_reduce_fusion.4 = s32[256]{0:T(256)S(1)} fusion(s32[256,512]{0,1:T(8,128)S(1)} %bitcast.97, pred[512,16]{1,0:T(8,128)(4,1)S(1)} %add_compare_fusion.4), kind=kLoop, calls=%fused_computation.7.clone.1 | loop fusion | flops 8388352 | bytes 533504 | tf_op jit(solution)/shard_map/while/body/eval_jaxpr/reduce_sum | solution.py:46
  92.4 2.8 fusion.43
  95.2 3.6 %select_reduce_fusion.4 = s32[256]{0:T(256)S(1)} fusion(s32[256,512]{0,1:T(8,128)S(1)} %bitcast.97, pred[512,16]{1,0:T(8,128)(4,1)S(1)} %add_compare_fusion.4), kind=kLoop, calls=%fused_computation.7.clone.1 | loop fusion | flops 8388352 | bytes 533504 | tf_op jit(solution)/shard_map/while/body/eval_jaxpr/reduce_sum | solution.py:46
  101.4 2.8 fusion.43
  104.2 3.6 %select_reduce_fusion.4 = s32[256]{0:T(256)S(1)} fusion(s32[256,512]{0,1:T(8,128)S(1)} %bitcast.97, pred[512,16]{1,0:T(8,128)(4,1)S(1)} %add_compare_fusion.4), kind=kLoop, calls=%fused_computation.7.clone.1 | loop fusion | flops 8388352 | bytes 533504 | tf_op jit(solution)/shard_map/while/body/eval_jaxpr/reduce_sum | solution.py:46
  110.4 2.8 fusion.43
  113.2 3.6 %select_reduce_fusion.4 = s32[256]{0:T(256)S(1)} fusion(s32[256,512]{0,1:T(8,128)S(1)} %bitcast.97, pred[512,16]{1,0:T(8,128)(4,1)S(1)} %add_compare_fusion.4), kind=kLoop, calls=%fused_computation.7.clone.1 | loop fusion | flops 8388352 | bytes 533504 | tf_op jit(solution)/shard_map/while/body/eval_jaxpr/reduce_sum | solution.py:46
  119.5 19.6 %all_to_all.10 = f32[2,1024,128]{1,2,0:T(8,128)S(1)} all-to-all(f32[2,1024,128]{1,2,0:T(8,128)S(1)} %bitcast.100), channel_id=1, replica_groups=mesh['dom'=32,'col'=2,'batch'=2] {'col'}, dimensions={0} | all-to-all | bytes 2097152 | tf_op jit(solution)/shard_map/all_to_all | solution.py:18
  139.4 8.0 %all_gather.24 = bf16[2048,128]{1,0:T(8,128)(2,1)S(1)} all-gather(bf16[1024,128]{1,0:T(8,128)(2,1)S(1)} %maximum_convert_fusion), channel_id=1, replica_groups=mesh['dom'=32,'col'=2,'batch'=2] {'batch'}, dimensions={0}, use_global_device_ids=true | all-gather | bytes 786432 | tf_op jit(solution)/shard_map/all_gather | solution.py:95
  149.1 4.5 %all-gather = bf16[2,86,128]{2,1,0:T(8,128)(2,1)S(1)} all-gather(bf16[1,86,128]{2,1,0:T(8,128)(2,1)S(1)} %bitcast.106), channel_id=1, replica_groups=mesh['dom'=32,'col'=2,'batch'=2] {'batch'}, dimensions={0}, use_global_device_ids=true | all-gather | bytes 66048 | tf_op jit(solution)/shard_map/all_gather | solution.py:106
  153.6 4.7 %all-gather.1 = bf16[2,86,128]{2,1,0:T(8,128)(2,1)S(1)} all-gather(bf16[1,86,128]{2,1,0:T(8,128)(2,1)S(1)} %bitcast.107), channel_id=1, replica_groups=mesh['dom'=32,'col'=2,'batch'=2] {'batch'}, dimensions={0}, use_global_device_ids=true | all-gather | bytes 66048 | tf_op jit(solution)/shard_map/all_gather | solution.py:107
  158.5 3.2 %gather_fusion.1 = bf16[1024,128]{1,0:T(8,128)(2,1)S(1)} fusion(bf16[2048,128]{1,0:T(8,128)(2,1)S(1)} %all_gather.24, s32[1024]{0:T(1024)S(1)} %fusion.18), kind=kCustom, calls=%fused_computation.1 | custom fusion | bytes 528384 | tf_op jit(solution)/shard_map/jit(_take)/gather | solution.py:104
  162.1 56.3 %all-gather.7.cloned.1.call-done = bf16[512,16384]{1,0:T(8,128)(2,1)} async-done(((bf16[16,16384]{1,0:T(8,128)(2,1)}), bf16[512,16384]{1,0:T(8,128)(2,1)}) %all-gather.7.cloned.1.call-update) | async-done | bytes 16777232 | tf_op jit(solution)/shard_map/all_gather | solution.py:100
  218.3 12.9 %gather_fusion.2 = bf16[64,16384]{1,0:T(8,128)(2,1)} fusion(bf16[512,16384]{1,0:T(8,128)(2,1)} %all-gather.7.cloned.1.call-done, s32[1024]{0:T(1024)S(1)} %pad_clamp_fusion), kind=kCustom, calls=%fused_computation.2 | custom fusion | bytes 4194560 | tf_op jit(solution)/shard_map/jit(_take)/gather | solution.py:57
  231.3 2.9 gather.20
  234.2 6.7 %select_select_fusion = bf16[8192,128]{1,0:T(8,128)(2,1)} fusion(bf16[8192,128]{1,0:T(8,128)(2,1)S(1)} %gather.20, pred[8192]{0:T(1024)(128)(4,1)S(1)} %get-tuple-element.103, pred[8192]{0:T(1024)(128)(4,1)S(1)} %get-tuple-element.104), kind=kLoop, calls=%fused_computation.29 | loop fusion | flops 2097152 | bytes 4210688 | tf_op jit(solution)/shard_map/jit(_where)/select_n | solution.py:58
  240.9 37.2 %while.21 = (s32[]{:T(128)}, bf16[4,256,128]{2,1,0:T(8,128)(2,1)S(1)}, s32[]{:T(128)}, s32[4,256,512]{2,1,0:T(8,128)}, bf16[8192,128]{1,0:T(8,128)(2,1)}, /*index=5*/s32[]{:T(128)}) while((s32[]{:T(128)}, bf16[4,256,128]{2,1,0:T(8,128)(2,1)S(1)}, s32[]{:T(128)}, s32[4,256,512]{2,1,0:T(8,128)}, bf16[8192,128]{1,0:T(8,128)(2,1)}, ...), condition=%wide.region_6.7_spmd, body=%wide.region_4.6_spmd.sunk | while | flops 553746688 | bytes 22253680 | solution.py:52
  245.2 3.6 %select_reduce_fusion.5 = s32[256]{0:T(256)S(1)} fusion(s32[256,512]{0,1:T(8,128)S(1)} %bitcast.99, pred[512,16]{1,0:T(8,128)(4,1)S(1)} %add_compare_fusion.5), kind=kLoop, calls=%fused_computation.20.clone.1 | loop fusion | flops 8388352 | bytes 533504 | tf_op jit(solution)/shard_map/while/body/eval_jaxpr/reduce_sum | solution.py:46
  251.6 2.8 fusion.47
  254.5 3.6 %select_reduce_fusion.5 = s32[256]{0:T(256)S(1)} fusion(s32[256,512]{0,1:T(8,128)S(1)} %bitcast.99, pred[512,16]{1,0:T(8,128)(4,1)S(1)} %add_compare_fusion.5), kind=kLoop, calls=%fused_computation.20.clone.1 | loop fusion | flops 8388352 | bytes 533504 | tf_op jit(solution)/shard_map/while/body/eval_jaxpr/reduce_sum | solution.py:46
  261.0 2.8 fusion.47
  263.8 3.6 %select_reduce_fusion.5 = s32[256]{0:T(256)S(1)} fusion(s32[256,512]{0,1:T(8,128)S(1)} %bitcast.99, pred[512,16]{1,0:T(8,128)(4,1)S(1)} %add_compare_fusion.5), kind=kLoop, calls=%fused_computation.20.clone.1 | loop fusion | flops 8388352 | bytes 533504 | tf_op jit(solution)/shard_map/while/body/eval_jaxpr/reduce_sum | solution.py:46
  273.1 3.6 %select_reduce_fusion.5 = s32[256]{0:T(256)S(1)} fusion(s32[256,512]{0,1:T(8,128)S(1)} %bitcast.99, pred[512,16]{1,0:T(8,128)(4,1)S(1)} %add_compare_fusion.5), kind=kLoop, calls=%fused_computation.20.clone.1 | loop fusion | flops 8388352 | bytes 533504 | tf_op jit(solution)/shard_map/while/body/eval_jaxpr/reduce_sum | solution.py:46
  278.5 23.8 %all_to_all.11 = f32[2,1024,172]{1,2,0:T(8,128)S(1)} all-to-all(f32[2,1024,172]{1,2,0:T(8,128)S(1)} %broadcast_in_dim.146), channel_id=1, replica_groups=mesh['dom'=32,'col'=2,'batch'=2] {'col'}, dimensions={0} | all-to-all | bytes 2818048 | tf_op jit(solution)/shard_map/all_to_all | solution.py:24
  (115 shorter events, 38.8 us)
Async XLA Ops:
  6.5 58.5 %all-gather.5.cloned.1.call-start = ((), (), s32[]{:S(2)}) async-start(), calls=%async_computation.2 | async-start | bytes 8650752 | tf_op jit(solution)/shard_map/all_gather | solution.py:81
  9.0 209.4 %all-gather.7.cloned.1.call-start = ((), (), s32[]{:S(2)}) async-start(), calls=%async_computation.3 | async-start | bytes 17301504 | tf_op jit(solution)/shard_map/all_gather | solution.py:100
  117.9 31.2 %copy-start.1 = (bf16[128,86]{0,1:T(8,128)(2,1)S(1)}, bf16[128,86]{0,1:T(8,128)(2,1)}, u32[]{:S(2)}) copy-start(bf16[128,86]{0,1:T(8,128)(2,1)} %param.22) | copy-start | bytes 66052
  117.9 35.7 %copy-start.2 = (bf16[128,86]{0,1:T(8,128)(2,1)S(1)}, bf16[128,86]{0,1:T(8,128)(2,1)}, u32[]{:S(2)}) copy-start(bf16[128,86]{0,1:T(8,128)(2,1)} %param.23) | copy-start | bytes 66052
  117.9 40.3 %copy-start.4 = (s32[1,64]{1,0:T(1,128)S(1)}, s32[1,64]{1,0:T(1,128)}, u32[]{:S(2)}) copy-start(s32[1,64]{1,0:T(1,128)} %param.24) | copy-start | bytes 772
  117.9 40.4 %copy-start.3 = (s32[1024]{0:T(1024)S(1)}, s32[1024]{0:T(1024)}, u32[]{:S(2)}) copy-start(s32[1024]{0:T(1024)} %param.27) | copy-start | bytes 12292
  242.3 6.5 %copy-start = (bf16[8192,128]{1,0:T(8,128)(2,1)S(1)}, bf16[8192,128]{1,0:T(8,128)(2,1)}, u32[]{:S(2)}) copy-start(bf16[8192,128]{1,0:T(8,128)(2,1)} %get-tuple-element.201) | copy-start | bytes 6291460 | tf_op jit(solution)/shard_map/while
  251.6 6.5 %copy-start = (bf16[8192,128]{1,0:T(8,128)(2,1)S(1)}, bf16[8192,128]{1,0:T(8,128)(2,1)}, u32[]{:S(2)}) copy-start(bf16[8192,128]{1,0:T(8,128)(2,1)} %get-tuple-element.201) | copy-start | bytes 6291460 | tf_op jit(solution)/shard_map/while
  260.9 6.5 %copy-start = (bf16[8192,128]{1,0:T(8,128)(2,1)S(1)}, bf16[8192,128]{1,0:T(8,128)(2,1)}, u32[]{:S(2)}) copy-start(bf16[8192,128]{1,0:T(8,128)(2,1)} %get-tuple-element.201) | copy-start | bytes 6291460 | tf_op jit(solution)/shard_map/while
  270.3 6.5 %copy-start = (bf16[8192,128]{1,0:T(8,128)(2,1)S(1)}, bf16[8192,128]{1,0:T(8,128)(2,1)}, u32[]{:S(2)}) copy-start(bf16[8192,128]{1,0:T(8,128)(2,1)} %get-tuple-element.201) | copy-start | bytes 6291460 | tf_op jit(solution)/shard_map/while
Sparse Core Ops, SparseCore 0:
  9.6 55.3 all-gather.4
  148.5 69.7 all-gather.6
where the time goes:
time: 311 us; the launch traced here: 310 us
  waiting for transfers between devices  97.9 us (31%)
  blocking collectives  69.7 us (22%)
  other arithmetic  68.5 us (22%)
  local copies, waits for them, and re-layouts  44.3 us (14%)
  between operations  15 us (5%)
  matrix products  14 us (5%)
    all_gather x1, waiting for transfers between devices, per_device(): lax.all_gather(front_blocks, 'dom', axis=0, tiled=True)  56.3 us
    all_gather x1, waiting for transfers between devices, per_device(): lax.all_gather(node_blocks, 'dom', axis=0, tiled=True)  41.6 us
    reduce_sum x8, other arithmetic, one_block(): degree = jnp.sum(dense_rows, axis=1).astype(jnp.float32)  28.7 us
    gather x4, local copies, waits for them, and re-layouts, pick_blocks(): jnp.take(arriving, jnp.clip(wanted, 0, arriving.shape[0] - 1), axis=0)  25.7 us
    all_to_all x1, blocking collectives, from_everyone(): return lax.all_to_all(copies, axis, split_axis=0, concat_axis=0, tiled=True)  23.8 us
    convert_element_type x8, other arithmetic, one_block(): dense_rows.astype(jnp.bfloat16)  22.2 us
    all_to_all x1, blocking collectives, sent_and_summed(): lax.all_to_all(in_blocks(shard, dim, devices), axis, 0, 0, tiled=True)  19.6 us
    select_n x2, other arithmetic, pick_blocks(): return jnp.where(inside[:, None], taken_rows, holding)  13.7 us
  transfers between devices with their start and end apart: 2, of which 2 were waited for; matrix products, arithmetic and copies ran while one was open for 3% of the time, Pallas kernels for 0%

commit v1 on v0

--- a/solution.py
+++ b/solution.py
@@ -96,9 +96,10 @@
     front_blocks = frontier.reshape(frontier.shape[0] // BLK, BLK * frontier.shape[1])
     wanted_second = need_second[0]
     empty_second = jnp.zeros((wanted_second.shape[0], front_blocks.shape[1]), jnp.bfloat16)
-    fetched_second = pick_blocks(
-        empty_second, wanted_second, lax.all_gather(front_blocks, "dom", axis=0, tiled=True)
+    members_all_launch = lambda local_block: jnp.concatenate(
+        lax.all_to_all(jnp.stack([local_block] * lax.axis_size("dom"), 0), "dom", 0, 0), 0
     )
+    fetched_second = pick_blocks(empty_second, wanted_second, members_all_launch(front_blocks))
     needed_second = fetched_second.reshape(-1, frontier.shape[1])
     near_second = mean_rows(adjacency_second, count_second[0] * BLK, needed_second)
     own_second = jnp.take(frontier, seed_rows, axis=0)

time: 311 us -> 458 us (1.47)
  waiting for transfers between devices: 97.9 us -> 241 us
  blocking collectives: 69.7 us -> 61.5 us
  starting transfers between devices: 0.04 us -> 5.76 us
  local copies, waits for them, and re-layouts: 44.3 us -> 49.5 us
    all_to_all x0 -> x1, waiting for transfers between devices: none -> 200 us  [per_device(): lax.all_to_all(jnp.stack([local_block] * lax.axis_size('dom'), 0), 'dom',...]
    all_gather x1 -> x0, waiting for transfers between devices: 56.3 us -> none  [per_device(): lax.all_gather(front_blocks, 'dom', axis=0, tiled=True)]
    all_to_all x1, blocking collectives: 23.8 us -> 15.5 us  [from_everyone(): return lax.all_to_all(copies, axis, split_axis=0, concat_axis=0, tiled=True)]
    another operation x0 -> x2, local copies, waits for them, and re-layouts: none -> 6.19 us  [per_device(): jnp.stack([local_block] * lax.axis_size('dom'), 0)]
    all_to_all x0 -> x1, starting transfers between devices: none -> 5.76 us  [per_device(): lax.all_to_all(jnp.stack([local_block] * lax.axis_size('dom'), 0), 'dom',...]
  transfers between devices with their start and end apart: 2 -> 2, of which waited for: 2 -> 2; matrix products, arithmetic and copies ran while one was open for 3% -> 2% of each run, Pallas kernels for 0% -> 0%
where the time goes in v1:
time: 458 us; the launch traced here: 456 us
  waiting for transfers between devices  241 us (53%)
  other arithmetic  68.5 us (15%)
  blocking collectives  61.5 us (13%)
  local copies, waits for them, and re-layouts  49.5 us (11%)
  between operations  14.9 us (3%)
  matrix products  14 us (3%)
  starting transfers between devices  5.76 us (1%)
    all_to_all x1, waiting for transfers between devices, per_device(): lax.all_to_all(jnp.stack([local_block] * lax.axis_size('dom'), 0), 'dom',...  200 us
    all_gather x1, waiting for transfers between devices, per_device(): lax.all_gather(node_blocks, 'dom', axis=0, tiled=True)  41.7 us
    reduce_sum x8, other arithmetic, one_block(): degree = jnp.sum(dense_rows, axis=1).astype(jnp.float32)  28.7 us
    gather x4, local copies, waits for them, and re-layouts, pick_blocks(): jnp.take(arriving, jnp.clip(wanted, 0, arriving.shape[0] - 1), axis=0)  25.7 us
    convert_element_type x8, other arithmetic, one_block(): dense_rows.astype(jnp.bfloat16)  22.2 us
    all_to_all x1, blocking collectives, sent_and_summed(): lax.all_to_all(in_blocks(shard, dim, devices), axis, 0, 0, tiled=True)  19.6 us
    all_to_all x1, blocking collectives, from_everyone(): return lax.all_to_all(copies, axis, split_axis=0, concat_axis=0, tiled=True)  15.5 us
    select_n x2, other arithmetic, pick_blocks(): return jnp.where(inside[:, None], taken_rows, holding)  13.7 us
  transfers between devices with their start and end apart: 2, of which 2 were waited for; matrix products, arithmetic and copies ran while one was open for 2% of the time, Pallas kernels for 0%

profile of v1, /device:TPU:0, one launch (start us, length us, event | category | flops | bytes accessed | tf_op | source)
XLA Modules:
  0.0 456.1 jit_solution(9602624572398264947)
XLA Ops:
  9.6 4.6 %all_gather.18 = bf16[64,256]{1,0:T(8,128)(2,1)S(1)} all-gather(bf16[64,128]{1,0:T(8,128)(2,1)} %param.17), channel_id=1, replica_groups=mesh['dom'=32,'col'=2,'batch'=2] {'batch'}, dimensions={1}, use_global_device_ids=true | all-gather | bytes 49152 | tf_op jit(solution)/shard_map/all_gather | solution.py:87
  14.3 4.6 %all_gather.20 = bf16[64,256]{1,0:T(8,128)(2,1)S(1)} all-gather(bf16[64,128]{1,0:T(8,128)(2,1)} %param.18), channel_id=1, replica_groups=mesh['dom'=32,'col'=2,'batch'=2] {'batch'}, dimensions={1}, use_global_device_ids=true | all-gather | bytes 49152 | tf_op jit(solution)/shard_map/all_gather | solution.py:88
  23.3 41.7 %all-gather.4.cloned.1.call-done = bf16[512,8192]{1,0:T(8,128)(2,1)} async-done(((bf16[16,8192]{1,0:T(8,128)(2,1)}), bf16[512,8192]{1,0:T(8,128)(2,1)}) %all-gather.4.cloned.1.call-update) | async-done | bytes 8388624 | tf_op jit(solution)/shard_map/all_gather | solution.py:81
  65.0 6.6 %gather_fusion = bf16[64,8192]{1,0:T(8,128)(2,1)S(1)} fusion(bf16[512,8192]{1,0:T(8,128)(2,1)} %all-gather.4.cloned.1.call-done, s32[1024]{0:T(1024)S(1)} %pad_clamp_fusion.1), kind=kCustom, calls=%fused_computation | custom fusion | bytes 2097408 | tf_op jit(solution)/shard_map/jit(_take)/gather | solution.py:57
  71.6 3.3 gather.17
  74.9 7.0 %select_select_fusion.1 = bf16[8192,64]{1,0:T(8,128)(2,1)S(1)} fusion(bf16[8192,64]{1,0:T(8,128)(2,1)} %gather.17, pred[8192]{0:T(1024)(128)(4,1)S(1)} %get-tuple-element.101, pred[8192]{0:T(1024)(128)(4,1)S(1)} %get-tuple-element.102), kind=kLoop, calls=%fused_computation.30 | loop fusion | flops 1048576 | bytes 2113536 | tf_op jit(solution)/shard_map/jit(_where)/select_n | solution.py:58
  81.9 36.0 %while.20 = (s32[]{:T(128)}, bf16[4,256,64]{1,2,0:T(8,128)(2,1)S(1)}, s32[]{:T(128)}, s32[4,256,512]{2,1,0:T(8,128)}, bf16[8192,64]{1,0:T(8,128)(2,1)S(1)}, /*index=5*/s32[]{:T(128)}) while((s32[]{:T(128)}, bf16[4,256,64]{1,2,0:T(8,128)(2,1)S(1)}, s32[]{:T(128)}, s32[4,256,512]{2,1,0:T(8,128)}, bf16[8192,64]{1,0:T(8,128)(2,1)S(1)}, ...), condition=%wide.region_2.3_spmd, body=%wide.region_0.2_spmd.sunk | while | flops 285278464 | bytes 13832277 | solution.py:52
  86.3 3.6 select_reduce_fusion.4
  95.2 3.6 select_reduce_fusion.4
  101.4 2.8 fusion.43
  104.2 3.6 select_reduce_fusion.4
  110.4 2.8 fusion.43
  113.2 3.6 select_reduce_fusion.4
  119.5 19.6 %all_to_all.15 = f32[2,1024,128]{1,2,0:T(8,128)S(1)} all-to-all(f32[2,1024,128]{1,2,0:T(8,128)S(1)} %bitcast.101), channel_id=1, replica_groups=mesh['dom'=32,'col'=2,'batch'=2] {'col'}, dimensions={0} | all-to-all | bytes 2097152 | tf_op jit(solution)/shard_map/all_to_all | solution.py:18
  139.3 8.0 %all_gather.21 = bf16[2048,128]{1,0:T(8,128)(2,1)S(1)} all-gather(bf16[1024,128]{1,0:T(8,128)(2,1)S(1)} %maximum_convert_fusion), channel_id=1, replica_groups=mesh['dom'=32,'col'=2,'batch'=2] {'batch'}, dimensions={0}, use_global_device_ids=true | all-gather | bytes 786432 | tf_op jit(solution)/shard_map/all_gather | solution.py:95
  147.6 6.0 %stack.3 = bf16[32,16,16384]{2,1,0:T(8,128)(2,1)} broadcast(bf16[16,16384]{1,0:T(8,128)(2,1)S(1)} %stack_reshape.2), dimensions={1,2} | broadcast | bytes 17301504 | tf_op jit(solution)/shard_map/stack | solution.py:100
  153.5 5.8 %all-to-all-start.1 = ((bf16[32,16,16384]{2,1,0:T(8,128)(2,1)}), bf16[32,16,16384]{2,1,0:T(8,128)(2,1)}, u32[]{:S(2)}, u32[]{:S(2)}) async-start(bf16[32,16,16384]{2,1,0:T(8,128)(2,1)} %stack.3), calls=%async_computation.1 | async-start | bytes 33554432 | tf_op jit(solution)/shard_map/all_to_all | solution.py:100
  160.0 4.5 all-gather
  164.5 4.7 %all-gather.1 = bf16[2,86,128]{2,1,0:T(8,128)(2,1)S(1)} all-gather(bf16[1,86,128]{2,1,0:T(8,128)(2,1)S(1)} %bitcast.108), channel_id=1, replica_groups=mesh['dom'=32,'col'=2,'batch'=2] {'batch'}, dimensions={0}, use_global_device_ids=true | all-gather | bytes 66048 | tf_op jit(solution)/shard_map/all_gather | solution.py:108
  169.3 3.2 gather_fusion.1
  173.0 199.6 %all-to-all-done.1 = bf16[32,16,16384]{2,1,0:T(8,128)(2,1)} async-done(((bf16[32,16,16384]{2,1,0:T(8,128)(2,1)}), bf16[32,16,16384]{2,1,0:T(8,128)(2,1)}, u32[]{:S(2)}, u32[]{:S(2)}) %all-to-all-start.1) | async-done | bytes 16777248 | tf_op jit(solution)/shard_map/all_to_all | solution.py:100
  372.6 12.9 %gather_fusion.2 = bf16[64,16384]{1,0:T(8,128)(2,1)} fusion(bf16[512,16384]{1,0:T(8,128)(2,1)} %bitcast.24, s32[1024]{0:T(1024)S(1)} %pad_clamp_fusion), kind=kCustom, calls=%fused_computation.2 | custom fusion | bytes 4194560 | tf_op jit(solution)/shard_map/jit(_take)/gather | solution.py:57
  385.5 2.9 gather.20
  388.4 6.7 %select_select_fusion = bf16[8192,128]{1,0:T(8,128)(2,1)} fusion(bf16[8192,128]{1,0:T(8,128)(2,1)S(1)} %gather.20, pred[8192]{0:T(1024)(128)(4,1)S(1)} %get-tuple-element.103, pred[8192]{0:T(1024)(128)(4,1)S(1)} %get-tuple-element.104), kind=kLoop, calls=%fused_computation.29 | loop fusion | flops 2097152 | bytes 4210688 | tf_op jit(solution)/shard_map/jit(_where)/select_n | solution.py:58
  395.1 37.2 %while.21 = (s32[]{:T(128)}, bf16[4,256,128]{2,1,0:T(8,128)(2,1)S(1)}, s32[]{:T(128)}, s32[4,256,512]{2,1,0:T(8,128)}, bf16[8192,128]{1,0:T(8,128)(2,1)}, /*index=5*/s32[]{:T(128)}) while((s32[]{:T(128)}, bf16[4,256,128]{2,1,0:T(8,128)(2,1)S(1)}, s32[]{:T(128)}, s32[4,256,512]{2,1,0:T(8,128)}, bf16[8192,128]{1,0:T(8,128)(2,1)}, ...), condition=%wide.region_6.7_spmd, body=%wide.region_4.6_spmd.sunk | while | flops 553746688 | bytes 22253680 | solution.py:52
  396.6 2.8 fusion.47
  399.4 3.6 select_reduce_fusion.5
  408.7 3.6 select_reduce_fusion.5
  415.2 2.8 fusion.47
  418.0 3.6 select_reduce_fusion.5
  427.4 3.6 select_reduce_fusion.5
  432.7 15.5 %all_to_all.16 = f32[2,1024,172]{1,2,0:T(8,128)S(1)} all-to-all(f32[2,1024,172]{1,2,0:T(8,128)S(1)} %broadcast_in_dim.146), channel_id=1, replica_groups=mesh['dom'=32,'col'=2,'batch'=2] {'col'}, dimensions={0} | all-to-all | bytes 2818048 | tf_op jit(solution)/shard_map/all_to_all | solution.py:24
  (115 shorter events, 43.5 us)
Async XLA Ops:
  6.5 58.5 %all-gather.4.cloned.1.call-start = ((), (), s32[]{:S(2)}) async-start(), calls=%async_computation.3 | async-start | bytes 8650752 | tf_op jit(solution)/shard_map/all_gather | solution.py:81
  153.5 6.4 %copy-start.1 = (bf16[128,86]{0,1:T(8,128)(2,1)S(1)}, bf16[128,86]{0,1:T(8,128)(2,1)}, u32[]{:S(2)}) copy-start(bf16[128,86]{0,1:T(8,128)(2,1)} %param.22) | copy-start | bytes 66052
  153.5 10.9 %copy-start.2 = (bf16[128,86]{0,1:T(8,128)(2,1)S(1)}, bf16[128,86]{0,1:T(8,128)(2,1)}, u32[]{:S(2)}) copy-start(bf16[128,86]{0,1:T(8,128)(2,1)} %param.23) | copy-start | bytes 66052
  153.5 15.6 %copy-start.4 = (s32[1,64]{1,0:T(1,128)S(1)}, s32[1,64]{1,0:T(1,128)}, u32[]{:S(2)}) copy-start(s32[1,64]{1,0:T(1,128)} %param.24) | copy-start | bytes 772
  153.5 15.7 %copy-start.3 = (s32[1024]{0:T(1024)S(1)}, s32[1024]{0:T(1024)}, u32[]{:S(2)}) copy-start(s32[1024]{0:T(1024)} %param.27) | copy-start | bytes 12292
  153.5 219.0 %all-to-all-start.1 = ((bf16[32,16,16384]{2,1,0:T(8,128)(2,1)}), bf16[32,16,16384]{2,1,0:T(8,128)(2,1)}, u32[]{:S(2)}, u32[]{:S(2)}) async-start(bf16[32,16,16384]{2,1,0:T(8,128)(2,1)} %stack.3), calls=%async_computation.1 | async-start | bytes 33554432 | tf_op jit(solution)/shard_map/all_to_all | solution.py:100
  396.6 6.5 %copy-start = (bf16[8192,128]{1,0:T(8,128)(2,1)S(1)}, bf16[8192,128]{1,0:T(8,128)(2,1)}, u32[]{:S(2)}) copy-start(bf16[8192,128]{1,0:T(8,128)(2,1)} %get-tuple-element.201) | copy-start | bytes 6291460 | tf_op jit(solution)/shard_map/while
  405.9 6.5 %copy-start = (bf16[8192,128]{1,0:T(8,128)(2,1)S(1)}, bf16[8192,128]{1,0:T(8,128)(2,1)}, u32[]{:S(2)}) copy-start(bf16[8192,128]{1,0:T(8,128)(2,1)} %get-tuple-element.201) | copy-start | bytes 6291460 | tf_op jit(solution)/shard_map/while
  415.2 6.5 %copy-start = (bf16[8192,128]{1,0:T(8,128)(2,1)S(1)}, bf16[8192,128]{1,0:T(8,128)(2,1)}, u32[]{:S(2)}) copy-start(bf16[8192,128]{1,0:T(8,128)(2,1)} %get-tuple-element.201) | copy-start | bytes 6291460 | tf_op jit(solution)/shard_map/while
  424.5 6.5 %copy-start = (bf16[8192,128]{1,0:T(8,128)(2,1)S(1)}, bf16[8192,128]{1,0:T(8,128)(2,1)}, u32[]{:S(2)}) copy-start(bf16[8192,128]{1,0:T(8,128)(2,1)} %get-tuple-element.201) | copy-start | bytes 6291460 | tf_op jit(solution)/shard_map/while
Sparse Core Ops, SparseCore 0:
  9.6 55.3 all-gather.3
